TPU v7x, 32 devices: a whole 2x2x4 slice. The times are simulated.
32 devices in a mesh: grp: 2 (over x), tm: 16 (over z, y, core).
Axes of the slice: x: 2, y: 2, z: 4, core: 2. Of those that a mesh axis runs over, the one named last changes fastest.
Arguments:
- samples: bfloat16 [16, 2097152], P('grp', 'tm'), parts along dimension 0, may hold values from -128 to 127, as said below
- filter_taps: bfloat16 [16, 8192], replicated, may hold values from -4 to 4
Outputs:
- channelized: bfloat16 [16, 2, 4096, 256], P('grp', None, 'tm'), parts along dimension 0
There are 2 independent parts, one for each index of `grp`. A program takes and returns all parts, laid end to end along the dimension named above; an argument that names none is the same for every part. Nothing has to cross between parts.
Inputs may be any that keep to these rules, and one draw needn't show every extreme that they name: `samples`: every sample is a whole number, as from an 8-bit converter.
All inputs are finite; a program needn't handle non-finite values.
Results may differ from a plain program's by a relative error of at most 0.007.
Values may be sent and summed in bfloat16 or wider, within the bound.
A program may use at most 128 MiB of HBM per device.

v0:
```python
import jax
import jax.numpy as jnp
from jax import lax
from jax.sharding import PartitionSpec as P

ROW_LEN = 128
target_level = 0.378
epsilon = 1e-06


def shifted(value, axis, by):
    size = lax.axis_size(axis)
    pairs = [(i, i + by) for i in range(size) if 0 <= i + by < size]
    return lax.ppermute(value, axis, pairs)


def tables(row_len, col_len):
    fft_len = row_len * col_len
    rows_a = jnp.arange(row_len, dtype=jnp.int32)
    cols_b = jnp.arange(col_len, dtype=jnp.int32)
    half_c = jnp.arange(col_len // 2, dtype=jnp.int32)
    angle_a = (
        2.0 * jnp.pi / row_len * (rows_a[:, None] * rows_a[None, :] % row_len).astype(jnp.float32)
    )
    angle_t = (
        2.0 * jnp.pi / fft_len * (cols_b[:, None] * rows_a[None, :] % fft_len).astype(jnp.float32)
    )
    angle_b = (
        2.0 * jnp.pi / col_len * (cols_b[:, None] * half_c[None, :] % col_len).astype(jnp.float32)
    )
    return (
        jnp.cos(angle_a).astype(jnp.bfloat16),
        jnp.sin(angle_a).astype(jnp.bfloat16),
        jnp.cos(angle_t),
        jnp.sin(angle_t),
        jnp.cos(angle_b).astype(jnp.bfloat16),
        jnp.sin(angle_b).astype(jnp.bfloat16),
    )


def transform(filtered):
    streams, frames, fft_len = filtered.shape
    col_len = fft_len // ROW_LEN
    cos_a, sin_a, cos_t, sin_t, cos_b, sin_b = tables(ROW_LEN, col_len)
    blocks = filtered.reshape(streams, frames, ROW_LEN, col_len)
    first_re = jnp.einsum("sfab,ad->sfbd", blocks, cos_a, preferred_element_type=jnp.float32)
    first_im = -jnp.einsum("sfab,ad->sfbd", blocks, sin_a, preferred_element_type=jnp.float32)
    twisted_re = (first_re * cos_t + first_im * sin_t).astype(jnp.bfloat16)
    twisted_im = (first_im * cos_t - first_re * sin_t).astype(jnp.bfloat16)
    spec_re = jnp.einsum(
        "sfbd,bc->scdf", twisted_re, cos_b, preferred_element_type=jnp.float32
    ) + jnp.einsum("sfbd,bc->scdf", twisted_im, sin_b, preferred_element_type=jnp.float32)
    spec_im = jnp.einsum(
        "sfbd,bc->scdf", twisted_im, cos_b, preferred_element_type=jnp.float32
    ) - jnp.einsum("sfbd,bc->scdf", twisted_re, sin_b, preferred_element_type=jnp.float32)
    return (spec_re.reshape(streams, -1, frames), spec_im.reshape(streams, -1, frames))


def on_device(samples, filter_taps):
    streams = samples.shape[0]
    tap_count, fft_len = filter_taps.shape
    frames = samples.shape[1] // fft_len
    signal = samples.reshape(streams, frames, fft_len)
    history = shifted(signal[:, frames - (tap_count - 1) :, :], "tm", 1)
    extended = jnp.concatenate([history, signal], axis=1)
    weights = filter_taps.astype(jnp.float32)
    filtered = jnp.zeros((streams, frames, fft_len), jnp.float32)
    for tap_index in range(tap_count):
        offset = tap_count - 1 - tap_index
        filtered = filtered + weights[tap_index] * extended[:, offset : offset + frames].astype(
            jnp.float32
        )
    filtered = filtered.astype(jnp.bfloat16)
    spec_re, spec_im = transform(filtered)
    real_part = spec_re.astype(jnp.bfloat16)
    imag_part = spec_im.astype(jnp.bfloat16)
    real_wide = real_part.astype(jnp.float32)
    imag_wide = imag_part.astype(jnp.float32)
    local_power = jnp.sum(real_wide * real_wide + imag_wide * imag_wide, axis=(1, 2))
    total_power = lax.psum(local_power, "tm")
    count = frames * lax.axis_size("tm") * spec_re.shape[1]
    gain = target_level / jnp.sqrt(total_power / count + epsilon)
    scaled = jnp.stack(
        [
            jnp.clip(real_wide * gain[:, None, None], -1.0, 1.0),
            jnp.clip(imag_wide * gain[:, None, None], -1.0, 1.0),
        ],
        axis=1,
    ).astype(jnp.bfloat16)
    result = lax.all_to_all(scaled, "tm", split_axis=2, concat_axis=3, tiled=True)
    return result


def solution(mesh):
    return jax.shard_map(
        on_device,
        mesh=mesh,
        in_specs=(P("grp", "tm"), P()),
        out_specs=P("grp", None, "tm", None),
        check_vma=False,
    )
```

profile of v0, /device:TPU:1, one launch (start us, length us, event | category | flops | bytes accessed | tf_op | source)
XLA Modules:
  0.0 244.5 jit_solution(3988610349749079119)
XLA Ops:
  0.0 0.0 copy-start.2
  0.0 0.0 copy-start.1
  0.0 1.8 slice.130
  1.8 4.5 %collective-permute-start = (bf16[8,15,8192]{2,0,1:T(8,128)(2,1)S(1)}, bf16[8,15,8192]{2,0,1:T(8,128)(2,1)S(1)}, u32[]{:S(2)}, u32[]{:S(2)}) collective-permute-start(bf16[8,15,8192]{2,0,1:T(8,128)(2,1)S(1)} %slice.130), channel_id=1, source_target_pairs={{0,1},{1,2},{2,3},{3,4},{4,5},{5,6},{6,7},{7,8},{8,9},{9,10},{10,1... | collective-permute-start | bytes 5898248 | tf_op jit(solution)/shard_map/ppermute | solution.py:14
  6.4 0.1 fusion.43
  6.5 0.0 copy-done.2
  6.5 0.5 fusion.80
  7.0 20.9 %collective-permute-done = bf16[8,15,8192]{2,0,1:T(8,128)(2,1)S(1)} collective-permute-done((bf16[8,15,8192]{2,0,1:T(8,128)(2,1)S(1)}, bf16[8,15,8192]{2,0,1:T(8,128)(2,1)S(1)}, u32[]{:S(2)}, u32[]{:S(2)}) %collective-permute-start) | collective-permute-done | bytes 1966112 | tf_op jit(solution)/shard_map/ppermute | solution.py:14
  27.9 0.0 copy-done.1
  27.9 8.7 %add_convert_fusion.1 = bf16[8,16,8192]{2,0,1:T(8,128)(2,1)S(1)} fusion(bf16[8,16,8192]{2,0,1:T(8,128)(2,1)S(1)} %bitcast.84, bf16[8,15,8192]{2,0,1:T(8,128)(2,1)S(1)} %collective-permute-done, f32[8192]{0:T(1024)S(1)} %bitcast.100, f32[8192]{0:T(1024)S(1)} %bitcast.99, f32[8192]{0:T(1024)S(1)} %bitcast.98, f32[8192]{0:T(1024)S(1)} %bitcast.97, ...), kind=kLoop, calls=%fused_computation.30 | loop fusion | flops 66060288 | bytes 6684672 | tf_op jit(solution)/shard_map/convert_element_type | solution.py:73
  36.6 1.2 copy.27
  37.8 5.5 %reshape.106 = bf16[8,16,128,64]{3,2,1,0:T(8,128)(2,1)} reshape(bf16[8,16,8192]{2,1,0:T(8,128)(2,1)S(1)} %copy.27) | data formatting | bytes 4194304 | tf_op jit(solution)/shard_map/reshape | solution.py:45
  43.3 0.0 copy-start
  43.3 3.7 %fusion.33 = f32[8,16,64,128]{3,2,1,0:T(8,128)S(1)} fusion(bf16[8,16,128,64]{3,2,1,0:T(8,128)(2,1)} %reshape.106), kind=kOutput, calls=%fused_computation.81 | convolution fusion | flops 268681216 | bytes 6291456 | tf_op jit(solution)/shard_map/sfab,ad->sfbd/dot_general | solution.py:47
  47.0 0.0 copy-done
  47.0 1.7 add_convert_fusion
  48.8 0.5 fusion.54
  49.3 0.5 fusion.52
  49.8 0.5 add_convert_fusion.2
  50.3 1.6 convert_bitcast_fusion
  51.9 0.8 fusion.1
  52.7 30.6 %psum.7 = f32[8]{0:T(128)S(1)} all-reduce(f32[8]{0:T(128)S(1)} %get-tuple-element.25), channel_id=1, replica_groups=mesh['grp'=2,'tm'=16] {'tm'}, use_global_device_ids=true, to_apply=%region_1.2 | all-reduce | flops 8 | bytes 64 | tf_op jit(solution)/shard_map/psum | solution.py:80
  83.4 1.8 reshape.107
  85.1 1.6 convert_bitcast_fusion.1
  86.7 2.7 %reshape.108 = f32[8,1,4096,16]{2,3,0,1:T(8,128)} reshape(f32[8,32,128,16]{2,1,3,0:T(8,128)} %convert_bitcast_fusion.1) | data formatting | bytes 4194304 | tf_op jit(solution)/shard_map/convert_element_type | solution.py:78
  89.5 2.0 fusion.19
  91.5 0.2 pad_maximum_fusion.1
  91.7 27.8 %copy.32 = bf16[8,2,4096,16]{3,1,0,2:T(2,128)(2,1)} copy(bf16[8,2,4096,16]{2,3,1,0:T(8,128)(2,1)S(1)} %pad_maximum_fusion.1) | data formatting | bytes 4194304 | tf_op jit(solution)/shard_map/stack | solution.py:83
  119.5 19.7 %reshape.113 = bf16[16,2,32768]{2,1,0:T(2,128)(2,1)S(1)} reshape(bf16[4096,8,2,16]{3,2,1,0:T(2,128)(2,1)} %bitcast.80) | data formatting | bytes 4194304
  139.3 51.1 %all_to_all.18 = bf16[16,2,32768]{2,1,0:T(2,128)(2,1)} all-to-all(bf16[16,2,32768]{2,1,0:T(2,128)(2,1)S(1)} %reshape.113), channel_id=1, replica_groups=mesh['grp'=2,'tm'=16] {'tm'}, dimensions={0} | all-to-all | bytes 4194304 | tf_op jit(solution)/shard_map/all_to_all | solution.py:90
  190.4 16.5 %reshape.114 = bf16[4096,8,2,16]{3,2,1,0:T(2,128)(2,1)} reshape(bf16[16,2,32768]{2,1,0:T(2,128)(2,1)} %all_to_all.18) | data formatting | bytes 4194304
  206.8 35.3 %copy.43 = bf16[8,2,16,256,16]{3,4,2,1,0:T(8,128)(2,1)S(1)} copy(bf16[8,2,16,256,16]{4,1,0,3,2:T(2,128)(2,1)} %bitcast.81) | data formatting | bytes 4194304 | tf_op jit(solution)/shard_map/all_to_all | solution.py:90
  242.1 2.4 copy.35
  (1 shorter events, 0.0 us)
Async XLA Ops:
  0.0 6.5 %copy-start.2 = (bf16[16,8192]{1,0:T(8,128)(2,1)S(1)}, bf16[16,8192]{1,0:T(8,128)(2,1)}, u32[]{:S(2)}) copy-start(bf16[16,8192]{1,0:T(8,128)(2,1)} %param.3) | copy-start | bytes 786436
  0.0 27.9 %copy-start.1 = (bf16[8,131072]{1,0:T(8,128)(2,1)S(1)}, bf16[8,131072]{1,0:T(8,128)(2,1)}, u32[]{:S(2)}) copy-start(bf16[8,131072]{1,0:T(8,128)(2,1)} %param.2) | copy-start | bytes 6291460
  1.8 26.1 %collective-permute-start = (bf16[8,15,8192]{2,0,1:T(8,128)(2,1)S(1)}, bf16[8,15,8192]{2,0,1:T(8,128)(2,1)S(1)}, u32[]{:S(2)}, u32[]{:S(2)}) collective-permute-start(bf16[8,15,8192]{2,0,1:T(8,128)(2,1)S(1)} %slice.130), channel_id=1, source_target_pairs={{0,1},{1,2},{2,3},{3,4},{4,5},{5,6},{6,7},{7,8},{8,9},{9,10},{10,1... | collective-permute-start | bytes 5898248 | tf_op jit(solution)/shard_map/ppermute | solution.py:14
  43.3 3.7 %copy-start = (bf16[8,16,128,64]{3,2,1,0:T(8,128)(2,1)S(1)}, bf16[8,16,128,64]{3,2,1,0:T(8,128)(2,1)}, u32[]{:S(2)}) copy-start(bf16[8,16,128,64]{3,2,1,0:T(8,128)(2,1)} %reshape.106) | copy-start | bytes 6291460
where the time goes:
time: 246 us; the launch traced here: 244 us
  local copies, waits for them, and re-layouts  115 us (47%)
  blocking collectives  81.7 us (33%)
  waiting for transfers between devices  20.9 us (8%)
  other arithmetic  14.3 us (6%)
  matrix products  7.76 us (3%)
  starting transfers between devices  4.53 us (2%)
    all_to_all x1, blocking collectives, on_device(): lax.all_to_all(scaled, 'tm', split_axis=2, concat_axis=3, tiled=True)  51.1 us
    all_to_all x2, local copies, waits for them, and re-layouts, on_device(): lax.all_to_all(scaled, 'tm', split_axis=2, concat_axis=3, tiled=True)  37.7 us
    unnamed x8, local copies, waits for them, and re-layouts  36.2 us
    psum x1, blocking collectives, on_device(): total_power = lax.psum(local_power, 'tm')  30.6 us
    another operation x1, local copies, waits for them, and re-layouts, on_device(): jnp.stack([jnp.clip(real_wide * gain[:, None, None], -1.0, 1.0), jnp.clip...  27.8 us
    ppermute x1, waiting for transfers between devices, shifted(): return lax.ppermute(value, axis, pairs)  20.9 us
    convert_element_type x1, other arithmetic, on_device(): filtered = filtered.astype(jnp.bfloat16)  8.7 us
    reshape x1, local copies, waits for them, and re-layouts, transform(): blocks = filtered.reshape(streams, frames, ROW_LEN, col_len)  5.54 us
  transfers between devices with their start and end apart: 1, of which 1 were waited for; matrix products, arithmetic and copies ran while one was open for 0% of the time, Pallas kernels for 0%

commit v1 on v0

--- a/solution.py
+++ b/solution.py
@@ -77,7 +77,11 @@
     real_wide = real_part.astype(jnp.float32)
     imag_wide = imag_part.astype(jnp.float32)
     local_power = jnp.sum(real_wide * real_wide + imag_wide * imag_wide, axis=(1, 2))
-    total_power = lax.psum(local_power, "tm")
+    total_power = local_power
+    for hop in (1, 2, 4, 8):
+        total_power = total_power + lax.ppermute(
+            total_power, "tm", [(dev, dev ^ hop) for dev in range(16)]
+        )
     count = frames * lax.axis_size("tm") * spec_re.shape[1]
     gain = target_level / jnp.sqrt(total_power / count + epsilon)
     scaled = jnp.stack(

time: 246 us -> 231 us (0.939)
  blocking collectives: 81.7 us -> 56.1 us
  starting transfers between devices: 4.53 us -> 12.1 us
  waiting for transfers between devices: 20.9 us -> 23.8 us
    psum x1 -> x0, blocking collectives: 30.6 us -> none  [on_device(): total_power = lax.psum(local_power, 'tm')]
    ppermute x0 -> x4, starting transfers between devices: none -> 7.55 us  [on_device(): lax.ppermute(total_power, 'tm', [(dev, dev ^ hop) for dev in range(16)])]
    all_to_all x1, blocking collectives: 51.1 us -> 56.1 us  [on_device(): lax.all_to_all(scaled, 'tm', split_axis=2, concat_axis=3, tiled=True)]
    ppermute x0 -> x4, waiting for transfers between devices: none -> 2.87 us  [on_device(): lax.ppermute(total_power, 'tm', [(dev, dev ^ hop) for dev in range(16)])]
  transfers between devices with their start and end apart: 1 -> 5, of which waited for: 1 -> 4; matrix products, arithmetic and copies ran while one was open for 0% -> 3% of each run, Pallas kernels for 0% -> 0%
where the time goes in v1:
time: 231 us; the launch traced here: 229 us
  local copies, waits for them, and re-layouts  115 us (50%)
  blocking collectives  56.1 us (24%)
  waiting for transfers between devices  23.8 us (10%)
  other arithmetic  14.3 us (6%)
  starting transfers between devices  12.1 us (5%)
  matrix products  7.76 us (3%)
    all_to_all x1, blocking collectives, on_device(): lax.all_to_all(scaled, 'tm', split_axis=2, concat_axis=3, tiled=True)  56.1 us
    all_to_all x2, local copies, waits for them, and re-layouts, on_device(): lax.all_to_all(scaled, 'tm', split_axis=2, concat_axis=3, tiled=True)  37.7 us
    unnamed x8, local copies, waits for them, and re-layouts  36.2 us
    another operation x1, local copies, waits for them, and re-layouts, on_device(): jnp.stack([jnp.clip(real_wide * gain[:, None, None], -1.0, 1.0), jnp.clip...  27.9 us
    ppermute x1, waiting for transfers between devices, shifted(): return lax.ppermute(value, axis, pairs)  20.9 us
    convert_element_type x1, other arithmetic, on_device(): filtered = filtered.astype(jnp.bfloat16)  8.7 us
    ppermute x4, starting transfers between devices, on_device(): lax.ppermute(total_power, 'tm', [(dev, dev ^ hop) for dev in range(16)])  7.55 us
    reshape x1, local copies, waits for them, and re-layouts, transform(): blocks = filtered.reshape(streams, frames, ROW_LEN, col_len)  5.54 us
  transfers between devices with their start and end apart: 5, of which 4 were waited for; matrix products, arithmetic and copies ran while one was open for 3% of the time, Pallas kernels for 0%

profile of v1, /device:TPU:1, one launch (start us, length us, event | category | flops | bytes accessed | tf_op | source)
XLA Modules:
  0.0 229.4 jit_solution(7298002660130416226)
XLA Ops:
  0.0 0.0 copy-start.2
  0.0 0.0 copy-start.1
  0.0 1.8 slice.130
  1.8 4.5 %collective-permute-start = (bf16[8,15,8192]{2,0,1:T(8,128)(2,1)S(1)}, bf16[8,15,8192]{2,0,1:T(8,128)(2,1)S(1)}, u32[]{:S(2)}, u32[]{:S(2)}) collective-permute-start(bf16[8,15,8192]{2,0,1:T(8,128)(2,1)S(1)} %slice.130), channel_id=1, source_target_pairs={{0,1},{1,2},{2,3},{3,4},{4,5},{5,6},{6,7},{7,8},{8,9},{9,10},{10,1... | collective-permute-start | bytes 5898248 | tf_op jit(solution)/shard_map/ppermute | solution.py:14
  6.4 0.1 fusion.43
  6.5 0.0 copy-done.2
  6.5 0.5 fusion.80
  7.0 20.9 %collective-permute-done = bf16[8,15,8192]{2,0,1:T(8,128)(2,1)S(1)} collective-permute-done((bf16[8,15,8192]{2,0,1:T(8,128)(2,1)S(1)}, bf16[8,15,8192]{2,0,1:T(8,128)(2,1)S(1)}, u32[]{:S(2)}, u32[]{:S(2)}) %collective-permute-start) | collective-permute-done | bytes 1966112 | tf_op jit(solution)/shard_map/ppermute | solution.py:14
  27.9 0.0 copy-done.1
  27.9 8.7 %add_convert_fusion.1 = bf16[8,16,8192]{2,0,1:T(8,128)(2,1)S(1)} fusion(bf16[8,16,8192]{2,0,1:T(8,128)(2,1)S(1)} %bitcast.84, bf16[8,15,8192]{2,0,1:T(8,128)(2,1)S(1)} %collective-permute-done, f32[8192]{0:T(1024)S(1)} %bitcast.100, f32[8192]{0:T(1024)S(1)} %bitcast.99, f32[8192]{0:T(1024)S(1)} %bitcast.98, f32[8192]{0:T(1024)S(1)} %bitcast.97, ...), kind=kLoop, calls=%fused_computation.30 | loop fusion | flops 66060288 | bytes 6684672 | tf_op jit(solution)/shard_map/convert_element_type | solution.py:73
  36.6 1.2 copy.27
  37.8 5.5 %reshape.106 = bf16[8,16,128,64]{3,2,1,0:T(8,128)(2,1)} reshape(bf16[8,16,8192]{2,1,0:T(8,128)(2,1)S(1)} %copy.27) | data formatting | bytes 4194304 | tf_op jit(solution)/shard_map/reshape | solution.py:45
  43.3 0.0 copy-start
  43.3 3.7 %fusion.33 = f32[8,16,64,128]{3,2,1,0:T(8,128)S(1)} fusion(bf16[8,16,128,64]{3,2,1,0:T(8,128)(2,1)} %reshape.106), kind=kOutput, calls=%fused_computation.81 | convolution fusion | flops 268681216 | bytes 6291456 | tf_op jit(solution)/shard_map/sfab,ad->sfbd/dot_general | solution.py:47
  47.0 0.0 copy-done
  47.0 1.7 add_convert_fusion
  48.8 0.5 fusion.54
  49.3 0.5 fusion.52
  49.8 0.5 add_convert_fusion.2
  50.3 1.6 convert_bitcast_fusion
  51.9 0.8 fusion.1
  52.7 0.0 collective-permute-start.1
  52.8 1.6 convert_bitcast_fusion.1
  54.4 1.7 reshape.108
  56.1 2.8 %reshape.107 = f32[8,1,4096,16]{2,3,0,1:T(8,128)} reshape(f32[8,32,128,16]{2,1,3,0:T(8,128)} %convert_bitcast_fusion) | data formatting | bytes 4194304 | tf_op jit(solution)/shard_map/convert_element_type | solution.py:77
  58.9 0.0 collective-permute-done.1
  58.9 2.6 %collective-permute-start.2 = (f32[8]{0:T(128)S(1)}, f32[8]{0:T(128)S(1)}, u32[]{:S(2)}, u32[]{:S(2)}) collective-permute-start(f32[8]{0:T(128)S(1)} %add.131), channel_id=1, source_target_pairs={{0,2},{1,3},{2,0},{3,1},{4,6},{5,7},{6,4},{7,5},{8,10},{9,11},{10,... | collective-permute-start | bytes 104 | tf_op jit(solution)/shard_map/ppermute | solution.py:82
  61.5 1.0 collective-permute-done.2
  62.5 2.4 %collective-permute-start.3 = (f32[8]{0:T(128)S(1)}, f32[8]{0:T(128)S(1)}, u32[]{:S(2)}, u32[]{:S(2)}) collective-permute-start(f32[8]{0:T(128)S(1)} %add.132), channel_id=1, source_target_pairs={{0,4},{1,5},{2,6},{3,7},{4,0},{5,1},{6,2},{7,3},{8,12},{9,13},{10,... | collective-permute-start | bytes 104 | tf_op jit(solution)/shard_map/ppermute | solution.py:82
  64.9 1.0 collective-permute-done.3
  65.9 2.5 %collective-permute-start.4 = (f32[8]{0:T(128)S(1)}, f32[8]{0:T(128)S(1)}, u32[]{:S(2)}, u32[]{:S(2)}) collective-permute-start(f32[8]{0:T(128)S(1)} %add.133), channel_id=1, source_target_pairs={{0,8},{1,9},{2,10},{3,11},{4,12},{5,13},{6,14},{7,15},{8,0},{9,1},... | collective-permute-start | bytes 104 | tf_op jit(solution)/shard_map/ppermute | solution.py:82
  68.4 1.0 collective-permute-done.4
  69.3 2.0 fusion.19
  71.4 0.2 pad_maximum_fusion.1
  71.6 27.9 %copy.32 = bf16[8,2,4096,16]{3,1,0,2:T(2,128)(2,1)} copy(bf16[8,2,4096,16]{2,3,1,0:T(8,128)(2,1)S(1)} %pad_maximum_fusion.1) | data formatting | bytes 4194304 | tf_op jit(solution)/shard_map/stack | solution.py:87
  99.5 19.7 %reshape.113 = bf16[16,2,32768]{2,1,0:T(2,128)(2,1)S(1)} reshape(bf16[4096,8,2,16]{3,2,1,0:T(2,128)(2,1)} %bitcast.80) | data formatting | bytes 4194304
  119.2 56.1 %all_to_all.18 = bf16[16,2,32768]{2,1,0:T(2,128)(2,1)} all-to-all(bf16[16,2,32768]{2,1,0:T(2,128)(2,1)S(1)} %reshape.113), channel_id=1, replica_groups=mesh['grp'=2,'tm'=16] {'tm'}, dimensions={0} | all-to-all | bytes 4194304 | tf_op jit(solution)/shard_map/all_to_all | solution.py:94
  175.3 16.5 %reshape.114 = bf16[4096,8,2,16]{3,2,1,0:T(2,128)(2,1)} reshape(bf16[16,2,32768]{2,1,0:T(2,128)(2,1)} %all_to_all.18) | data formatting | bytes 4194304
  191.7 35.3 %copy.43 = bf16[8,2,16,256,16]{3,4,2,1,0:T(8,128)(2,1)S(1)} copy(bf16[8,2,16,256,16]{4,1,0,3,2:T(2,128)(2,1)} %bitcast.81) | data formatting | bytes 4194304 | tf_op jit(solution)/shard_map/all_to_all | solution.py:94
  227.0 2.4 %copy.35 = bf16[8,2,256,256]{3,2,1,0:T(8,128)(2,1)} copy(bf16[8,2,256,256]{2,3,1,0:T(8,128)(2,1)S(1)} %bitcast.82) | data formatting | bytes 4194304 | tf_op jit(solution)/shard_map/all_to_all | solution.py:94
  (4 shorter events, 0.0 us)
Async XLA Ops:
  0.0 6.5 %copy-start.2 = (bf16[16,8192]{1,0:T(8,128)(2,1)S(1)}, bf16[16,8192]{1,0:T(8,128)(2,1)}, u32[]{:S(2)}) copy-start(bf16[16,8192]{1,0:T(8,128)(2,1)} %param.3) | copy-start | bytes 786436
  0.0 27.9 %copy-start.1 = (bf16[8,131072]{1,0:T(8,128)(2,1)S(1)}, bf16[8,131072]{1,0:T(8,128)(2,1)}, u32[]{:S(2)}) copy-start(bf16[8,131072]{1,0:T(8,128)(2,1)} %param.2) | copy-start | bytes 6291460
  1.8 26.1 %collective-permute-start = (bf16[8,15,8192]{2,0,1:T(8,128)(2,1)S(1)}, bf16[8,15,8192]{2,0,1:T(8,128)(2,1)S(1)}, u32[]{:S(2)}, u32[]{:S(2)}) collective-permute-start(bf16[8,15,8192]{2,0,1:T(8,128)(2,1)S(1)} %slice.130), channel_id=1, source_target_pairs={{0,1},{1,2},{2,3},{3,4},{4,5},{5,6},{6,7},{7,8},{8,9},{9,10},{10,1... | collective-permute-start | bytes 5898248 | tf_op jit(solution)/shard_map/ppermute | solution.py:14
  43.3 3.7 %copy-start = (bf16[8,16,128,64]{3,2,1,0:T(8,128)(2,1)S(1)}, bf16[8,16,128,64]{3,2,1,0:T(8,128)(2,1)}, u32[]{:S(2)}) copy-start(bf16[8,16,128,64]{3,2,1,0:T(8,128)(2,1)} %reshape.106) | copy-start | bytes 6291460
  52.7 6.2 %collective-permute-start.1 = (f32[8]{0:T(128)S(1)}, f32[8]{0:T(128)S(1)}, u32[]{:S(2)}, u32[]{:S(2)}) collective-permute-start(f32[8]{0:T(128)S(1)} %get-tuple-element.25), channel_id=1, source_target_pairs={{0,1},{1,0},{2,3},{3,2},{4,5},{5,4},{6,7},{7,6},{8,9},{9,8},{10,11... | collective-permute-start | bytes 104 | tf_op jit(solution)/shard_map/ppermute | solution.py:82
  58.9 3.6 %collective-permute-start.2 = (f32[8]{0:T(128)S(1)}, f32[8]{0:T(128)S(1)}, u32[]{:S(2)}, u32[]{:S(2)}) collective-permute-start(f32[8]{0:T(128)S(1)} %add.131), channel_id=1, source_target_pairs={{0,2},{1,3},{2,0},{3,1},{4,6},{5,7},{6,4},{7,5},{8,10},{9,11},{10,... | collective-permute-start | bytes 104 | tf_op jit(solution)/shard_map/ppermute | solution.py:82
  62.5 3.4 %collective-permute-start.3 = (f32[8]{0:T(128)S(1)}, f32[8]{0:T(128)S(1)}, u32[]{:S(2)}, u32[]{:S(2)}) collective-permute-start(f32[8]{0:T(128)S(1)} %add.132), channel_id=1, source_target_pairs={{0,4},{1,5},{2,6},{3,7},{4,0},{5,1},{6,2},{7,3},{8,12},{9,13},{10,... | collective-permute-start | bytes 104 | tf_op jit(solution)/shard_map/ppermute | solution.py:82
  65.9 3.4 %collective-permute-start.4 = (f32[8]{0:T(128)S(1)}, f32[8]{0:T(128)S(1)}, u32[]{:S(2)}, u32[]{:S(2)}) collective-permute-start(f32[8]{0:T(128)S(1)} %add.133), channel_id=1, source_target_pairs={{0,8},{1,9},{2,10},{3,11},{4,12},{5,13},{6,14},{7,15},{8,0},{9,1},... | collective-permute-start | bytes 104 | tf_op jit(solution)/shard_map/ppermute | solution.py:82
